TPU v7x, 128 devices: a whole 4x4x4 slice. The times are simulated.
128 devices in a mesh: tiles: 32 (over x, y, core), reps: 4 (over z).
Axes of the slice: x: 4, y: 4, z: 4, core: 2. Of those that a mesh axis runs over, the one named last changes fastest.
Arguments:
- tiles_w: bfloat16 [4096, 128, 128], P('tiles'), may hold values from 0.0001 to 4
- tile_worker: int32 [4096], P('tiles'), may hold values from 0 to 15
- tile_owner: int32 [4096], P('tiles'), may hold values from 0 to 31
- owner_block: int32 [32, 32], P('tiles'), may hold values from 0 to 1
- worker_base: float32 [65536], P('tiles'), may hold values from -6 to 6
- worker_noise: float32 [65536], P('tiles'), may hold values from 0.2 to 1.5
- worker_cluster: int32 [65536], P('tiles'), may hold values from 0 to 255
- firm_base: float32 [8192], P('tiles'), may hold values from -6 to 6
- firm_noise: float32 [8192], P('tiles'), may hold values from 0.2 to 1.5
- firm_cluster: int32 [8192], P('tiles'), may hold values from 0 to 255
- signs: int32 [256, 256], P('reps'), may hold values from 0 to 1
- covariates: float32 [8192, 512], P('tiles'), may hold values from -0.0625 to 0.0625
- whitening: float32 [512, 512], replicated, may hold values from -0.25 to 0.25
Outputs:
- worker_effect: float32 [256, 65536], P('reps', 'tiles')
- firm_effect: float32 [256, 8192], P('reps', 'tiles')
- coefficients: float32 [256, 512], P('reps')
- covariance: float32 [512, 512], P('tiles')
Inputs may be any that keep to these rules, and one draw needn't show every extreme that they name: `tile_worker`: local worker block of each tile. `tile_owner`: owner of each tile's firm block. `owner_block`: firm block among the owner's 2 blocks. `signs`: a bit that gives the sign 2 b - 1.
All inputs are finite; a program needn't handle non-finite values.
Results may differ from a plain program's by a relative error of at most 0.0023.
Values may be sent and summed in bfloat16 or wider, within the bound.
No kernel may reach another device: no remote copies, remote signals or barrier semaphores. Data moves between devices by JAX's collectives and lax.ppermute only.
A program may use at most 64 MiB of HBM per device.

v0:
```python
import jax
import jax.numpy as jnp
from jax import lax
from jax.sharding import PartitionSpec as P

WORK_BLOCKS = 16
FIRM_BLOCKS = 2
SWEEPS = 6
spectral_bound = 0.8


def chebyshev_weights(sweep_count):
    weights = [1.0]
    weights.append(1.0 / (1.0 - 0.5 * spectral_bound * spectral_bound))
    while len(weights) < sweep_count:
        weights.append(1.0 / (1.0 - 0.25 * spectral_bound * spectral_bound * weights[-1]))
    return weights


def one_hot_rows(indices, row_count):
    return (indices[None, :] == jnp.arange(row_count, dtype=jnp.int32)[:, None]).astype(jnp.float32)


def wild_outcome(base_value, noise_scale, cluster, flip_table):
    clusters_hot = (
        cluster[None, :] == jnp.arange(flip_table.shape[1], dtype=jnp.int32)[:, None]
    ).astype(jnp.bfloat16)
    flip_values = jnp.dot(flip_table, clusters_hot, preferred_element_type=jnp.float32)
    return base_value[None, :] + noise_scale[None, :] * flip_values


def body(
    tiles_w,
    tile_worker,
    tile_owner,
    owner_block,
    worker_base,
    worker_noise,
    worker_cluster,
    firm_base,
    firm_noise,
    firm_cluster,
    signs,
    covariates,
    whitening,
):
    highest = lax.Precision.HIGHEST
    owners_count = lax.axis_size("tiles")
    tile_cells = tiles_w.shape[1]
    replicas_here = signs.shape[0]
    flip_table = (2 * signs - 1).astype(jnp.bfloat16)
    worker_outcome = wild_outcome(worker_base, worker_noise, worker_cluster, flip_table).reshape(
        replicas_here, WORK_BLOCKS, tile_cells
    )
    firm_outcome = wild_outcome(firm_base, firm_noise, firm_cluster, flip_table).reshape(
        replicas_here, FIRM_BLOCKS, tile_cells
    )
    row_mass = jnp.sum(tiles_w, axis=2, dtype=jnp.float32)
    col_mass = jnp.sum(tiles_w, axis=1, dtype=jnp.float32)
    worker_hot = one_hot_rows(tile_worker, WORK_BLOCKS)
    worker_scale = 1.0 + jnp.einsum("bt,tw->bw", worker_hot, row_mass, precision=highest)
    owner_hot = one_hot_rows(tile_owner, owners_count)
    my_blocks = owner_block[0]
    tile_block = tile_owner * FIRM_BLOCKS + jnp.sum(
        jnp.where(owner_hot > 0, my_blocks[:, None], 0), axis=0
    )
    dense_hot = one_hot_rows(tile_block, owners_count * FIRM_BLOCKS)
    firm_mass = lax.psum_scatter(
        jnp.einsum("nt,tf->nf", dense_hot, col_mass, precision=highest),
        "tiles",
        scatter_dimension=0,
        tiled=True,
    )
    firm_scale = 1.0 + firm_mass
    omegas = chebyshev_weights(SWEEPS)
    firm_older = jnp.zeros((replicas_here, FIRM_BLOCKS, tile_cells), jnp.float32)
    firm_newer = firm_older
    firm_now = firm_older
    worker_now = worker_outcome
    tile_firm = None
    for sweep_index in range(SWEEPS):
        if sweep_index == 0:
            worker_now = worker_outcome
        else:
            pulled = jnp.einsum(
                "twf,rtf->rtw", tiles_w, tile_firm, preferred_element_type=jnp.float32
            )
            worker_sum = jnp.einsum("bt,rtw->rbw", worker_hot, pulled, precision=highest)
            worker_now = worker_outcome - worker_sum / worker_scale[None]
        worker_round = worker_now.astype(jnp.bfloat16)
        tile_values = jnp.take(worker_round, tile_worker, axis=1)
        pushed = jnp.einsum(
            "twf,rtw->rtf", tiles_w, tile_values, preferred_element_type=jnp.float32
        )
        firm_sum = lax.psum_scatter(
            jnp.einsum("nt,rtf->rnf", dense_hot, pushed, precision=highest),
            "tiles",
            scatter_dimension=1,
            tiled=True,
        )
        firm_target = firm_outcome - firm_sum / firm_scale[None]
        firm_now = firm_older + omegas[sweep_index] * (firm_target - firm_older)
        firm_older, firm_newer = (firm_newer, firm_now)
        if sweep_index + 1 < SWEEPS:
            firm_round = firm_now.astype(jnp.bfloat16)
            every_firm = lax.all_gather(firm_round, "tiles", axis=1, tiled=True)
            tile_firm = jnp.take(every_firm, tile_block, axis=1)
    worker_effect = worker_now.reshape(replicas_here, WORK_BLOCKS * tile_cells)
    firm_flat = firm_now.reshape(replicas_here, FIRM_BLOCKS * tile_cells)
    mixing = jnp.dot(covariates, whitening.T, precision=highest)
    local_term = jnp.dot(firm_flat, mixing, precision=highest)
    summed = lax.psum(local_term, "tiles")
    share_rows = summed.shape[1] // owners_count
    own_columns = lax.dynamic_slice_in_dim(
        summed, lax.axis_index("tiles") * share_rows, share_rows, 1
    )
    moment = jnp.dot(own_columns.T, summed, precision=highest)
    covariance = lax.psum(moment, "reps") / (replicas_here * lax.axis_size("reps"))
    return (worker_effect, firm_flat, summed, covariance)


def solution(mesh):
    placed = (
        P("tiles", None, None),
        P("tiles"),
        P("tiles"),
        P("tiles", None),
        P("tiles"),
        P("tiles"),
        P("tiles"),
        P("tiles"),
        P("tiles"),
        P("tiles"),
        P("reps", None),
        P("tiles", None),
        P(),
    )
    return jax.shard_map(
        body,
        mesh=mesh,
        in_specs=placed,
        out_specs=(P("reps", "tiles"), P("reps", "tiles"), P("reps", None), P("tiles", None)),
        check_vma=False,
    )
```

profile of v0, /device:TPU:6, one launch (start us, length us, event | category | flops | bytes accessed | tf_op | source)
XLA Modules:
  0.0 1033.3 jit_solution(7390925900868006559)
XLA Ops:
  16.6 4.2 fusion.56
  28.9 109.8 %all-reduce = f32[64,128]{1,0:T(8,128)S(1)} all-reduce(f32[64,128]{1,0:T(8,128)S(1)} %fusion.164), channel_id=3, replica_groups=mesh['tiles'=32,'reps'=4] {'tiles'}, use_global_device_ids=true, to_apply=%region_3.0.clone | all-reduce | flops 8192 | bytes 65536
  140.8 57.8 %all-gather.6.cloned.1.call-done = bf16[64,64,128]{2,0,1:T(8,128)(2,1)} async-done(((bf16[64,2,128]{2,0,1:T(8,128)(2,1)}), bf16[64,64,128]{2,0,1:T(8,128)(2,1)}) %all-gather.6.cloned.1.call-update) | async-done | bytes 1048592 | tf_op jit(solution)/shard_map/all_gather | solution.py:106
  202.0 5.8 convolution_bitcast_fusion.9
  217.9 4.2 fusion.59
  225.1 78.4 %reduce-scatter.9.cloned.1.call-done = f32[64,2,128]{2,0,1:T(8,128)} async-done(((f32[64,64,128]{2,0,1:T(8,128)}), f32[64,2,128]{2,0,1:T(8,128)}) %reduce-scatter.9.cloned.1.call-update) | async-done | bytes 65552 | tf_op jit(solution)/shard_map/reduce_scatter | solution.py:95
  305.0 43.0 %all-gather.8.cloned.1.call-done = bf16[64,64,128]{2,0,1:T(8,128)(2,1)} async-done(((bf16[64,2,128]{2,0,1:T(8,128)(2,1)}), bf16[64,64,128]{2,0,1:T(8,128)(2,1)}) %all-gather.8.cloned.1.call-update) | async-done | bytes 1048592 | tf_op jit(solution)/shard_map/all_gather | solution.py:106
  351.3 5.8 convolution_bitcast_fusion.7
  367.3 4.2 fusion.62
  374.2 78.4 %reduce-scatter.11.cloned.1.call-done = f32[64,2,128]{2,0,1:T(8,128)} async-done(((f32[64,64,128]{2,0,1:T(8,128)}), f32[64,2,128]{2,0,1:T(8,128)}) %reduce-scatter.11.cloned.1.call-update) | async-done | bytes 65552 | tf_op jit(solution)/shard_map/reduce_scatter | solution.py:95
  454.2 43.0 %all-gather.10.cloned.1.call-done = bf16[64,64,128]{2,0,1:T(8,128)(2,1)} async-done(((bf16[64,2,128]{2,0,1:T(8,128)(2,1)}), bf16[64,64,128]{2,0,1:T(8,128)(2,1)}) %all-gather.10.cloned.1.call-update) | async-done | bytes 1048592 | tf_op jit(solution)/shard_map/all_gather | solution.py:106
  500.5 5.7 convolution_bitcast_fusion.5
  516.4 4.2 fusion.65
  523.6 78.4 %reduce-scatter.13.cloned.1.call-done = f32[64,2,128]{2,0,1:T(8,128)} async-done(((f32[64,64,128]{2,0,1:T(8,128)}), f32[64,2,128]{2,0,1:T(8,128)}) %reduce-scatter.13.cloned.1.call-update) | async-done | bytes 65552 | tf_op jit(solution)/shard_map/reduce_scatter | solution.py:95
  603.5 43.1 %all-gather.12.cloned.1.call-done = bf16[64,64,128]{2,0,1:T(8,128)(2,1)} async-done(((bf16[64,2,128]{2,0,1:T(8,128)(2,1)}), bf16[64,64,128]{2,0,1:T(8,128)(2,1)}) %all-gather.12.cloned.1.call-update) | async-done | bytes 1048592 | tf_op jit(solution)/shard_map/all_gather | solution.py:106
  650.0 5.8 convolution_bitcast_fusion.3
  665.9 4.2 fusion.68
  672.9 78.4 %reduce-scatter.15.cloned.1.call-done = f32[64,2,128]{2,0,1:T(8,128)} async-done(((f32[64,64,128]{2,0,1:T(8,128)}), f32[64,2,128]{2,0,1:T(8,128)}) %reduce-scatter.15.cloned.1.call-update) | async-done | bytes 65552 | tf_op jit(solution)/shard_map/reduce_scatter | solution.py:95
  752.8 43.0 %all-gather.14.cloned.1.call-done = bf16[64,64,128]{2,0,1:T(8,128)(2,1)} async-done(((bf16[64,2,128]{2,0,1:T(8,128)(2,1)}), bf16[64,64,128]{2,0,1:T(8,128)(2,1)}) %all-gather.14.cloned.1.call-update) | async-done | bytes 1048592 | tf_op jit(solution)/shard_map/all_gather | solution.py:106
  799.1 5.8 convolution_bitcast_fusion.1
  815.1 4.2 fusion.71
  824.1 76.3 %reduce-scatter.17.cloned.1.call-done = f32[64,2,128]{2,0,1:T(8,128)} async-done(((f32[64,64,128]{2,0,1:T(8,128)}), f32[64,2,128]{2,0,1:T(8,128)}) %reduce-scatter.17.cloned.1.call-update) | async-done | bytes 65552 | tf_op jit(solution)/shard_map/reduce_scatter | solution.py:95
  903.4 102.1 %all-reduce.3.cloned.1.call-done = f32[64,512]{1,0:T(8,128)} async-done(((f32[64,512]{1,0:T(8,128)}), f32[64,512]{1,0:T(8,128)}) %all-reduce.3.cloned.1.call-update) | async-done | bytes 131088 | tf_op jit(solution)/shard_map/psum | solution.py:112
  1006.8 17.3 %psum.15 = f32[16,512]{1,0:T(8,128)S(1)} all-reduce(f32[16,512]{1,0:T(8,128)S(1)} %fusion.162), channel_id=1, replica_groups=mesh['tiles'=32,'reps'=4] {'reps'}, use_global_device_ids=true, to_apply=%region_11.14 | all-reduce | flops 8192 | bytes 65536 | tf_op jit(solution)/shard_map/psum | solution.py:118
  (113 shorter events, 115.5 us)
Async XLA Ops:
  7.2 814.9 %copy-start = (f32[512,512]{1,0:T(8,128)S(1)}, f32[512,512]{1,0:T(8,128)}, u32[]{:S(2)}) copy-start(f32[512,512]{1,0:T(8,128)} %param.29) | copy-start | bytes 3145732
  7.2 3.1 copy-start.11
  7.2 3.1 copy-start.6
  7.2 131.7 %reduce-scatter.7.cloned.1.call-start = ((), (), s32[]{:S(2)}) async-start(), calls=%async_computation.6 | async-start | bytes 2162688 | tf_op jit(solution)/shard_map/reduce_scatter | solution.py:95
  23.4 175.2 %all-gather.6.cloned.1.call-start = ((), (), s32[]{:S(2)}) async-start(), calls=%async_computation.7 | async-start | bytes 1081344 | tf_op jit(solution)/shard_map/all_gather | solution.py:106
  25.2 113.4 %copy-start.7 = (s32[64,256]{1,0:T(8,128)S(1)}, s32[64,256]{1,0:T(8,128)}, u32[]{:S(2)}) copy-start(s32[64,256]{1,0:T(8,128)} %param.27) | copy-start | bytes 196612
  25.2 113.4 %copy-start.8 = (s32[256]{0:T(256)S(1)}, s32[256]{0:T(256)}, u32[]{:S(2)}) copy-start(s32[256]{0:T(256)} %param.26) | copy-start | bytes 3076
  25.2 113.4 %copy-start.9 = (f32[256]{0:T(256)S(1)}, f32[256]{0:T(256)}, u32[]{:S(2)}) copy-start(f32[256]{0:T(256)} %param.25) | copy-start | bytes 3076
  25.3 113.4 %copy-start.10 = (f32[256]{0:T(256)S(1)}, f32[256]{0:T(256)}, u32[]{:S(2)}) copy-start(f32[256]{0:T(256)} %param.24) | copy-start | bytes 3076
  25.3 115.4 %copy-start.5 = (s32[128]{0:T(128)S(1)}, s32[128]{0:T(128)}, u32[]{:S(2)}) copy-start(s32[128]{0:T(128)} %param.18) | copy-start | bytes 1540
  140.4 163.1 %reduce-scatter.9.cloned.1.call-start = ((), (), s32[]{:S(2)}) async-start(), calls=%async_computation.8 | async-start | bytes 2162688 | tf_op jit(solution)/shard_map/reduce_scatter | solution.py:95
  225.0 122.9 %all-gather.8.cloned.1.call-start = ((), (), s32[]{:S(2)}) async-start(), calls=%async_computation.9 | async-start | bytes 1081344 | tf_op jit(solution)/shard_map/all_gather | solution.py:106
  305.0 147.6 %reduce-scatter.11.cloned.1.call-start = ((), (), s32[]{:S(2)}) async-start(), calls=%async_computation.10 | async-start | bytes 2162688 | tf_op jit(solution)/shard_map/reduce_scatter | solution.py:95
  374.2 78.4 %copy-start.2 = (f32[64,2,128]{2,0,1:T(8,128)S(1)}, f32[64,2,128]{2,0,1:T(8,128)}, u32[]{:S(2)}) copy-start(f32[64,2,128]{2,0,1:T(8,128)} %reduce-scatter.7.cloned.1.call-done) | copy-start | bytes 196612
  374.2 122.9 %all-gather.10.cloned.1.call-start = ((), (), s32[]{:S(2)}) async-start(), calls=%async_computation.11 | async-start | bytes 1081344 | tf_op jit(solution)/shard_map/all_gather | solution.py:106
  454.1 147.9 %reduce-scatter.13.cloned.1.call-start = ((), (), s32[]{:S(2)}) async-start(), calls=%async_computation.12 | async-start | bytes 2162688 | tf_op jit(solution)/shard_map/reduce_scatter | solution.py:95
  523.5 78.4 %copy-start.3 = (f32[64,2,128]{2,0,1:T(8,128)S(1)}, f32[64,2,128]{2,0,1:T(8,128)}, u32[]{:S(2)}) copy-start(f32[64,2,128]{2,0,1:T(8,128)} %reduce-scatter.9.cloned.1.call-done) | copy-start | bytes 196612
  523.6 123.1 %all-gather.12.cloned.1.call-start = ((), (), s32[]{:S(2)}) async-start(), calls=%async_computation.13 | async-start | bytes 1081344 | tf_op jit(solution)/shard_map/all_gather | solution.py:106
  603.5 147.8 %reduce-scatter.15.cloned.1.call-start = ((), (), s32[]{:S(2)}) async-start(), calls=%async_computation.14 | async-start | bytes 2162688 | tf_op jit(solution)/shard_map/reduce_scatter | solution.py:95
  672.9 122.9 %all-gather.14.cloned.1.call-start = ((), (), s32[]{:S(2)}) async-start(), calls=%async_computation.15 | async-start | bytes 1081344 | tf_op jit(solution)/shard_map/all_gather | solution.py:106
  752.8 147.7 %reduce-scatter.17.cloned.1.call-start = ((), (), s32[]{:S(2)}) async-start(), calls=%async_computation.16 | async-start | bytes 2162688 | tf_op jit(solution)/shard_map/reduce_scatter | solution.py:95
  822.0 1.0 copy-start.1
  822.0 183.5 %all-reduce.3.cloned.1.call-start = ((), (), s32[]{:S(2)}) async-start(), calls=%async_computation.17 | async-start | bytes 262144 | tf_op jit(solution)/shard_map/psum | solution.py:112
  901.3 124.9 %copy-start.4 = (f32[64,256]{1,0:T(8,128)}, f32[64,256]{1,0:T(8,128)S(1)}, u32[]{:S(2)}) copy-start(f32[64,256]{1,0:T(8,128)S(1)} %copy_bitcast_fusion.1) | copy-start | bytes 196612
  (1 other events, 0.7 us)
Sparse Core Ops, SparseCore 0:
  23.5 80.7 reduce-scatter.6
  140.5 58.0 all-gather.5
  225.2 78.2 reduce-scatter.8
  306.1 41.7 all-gather.7
  374.3 78.2 reduce-scatter.10
  455.3 41.7 all-gather.9
  523.7 78.2 reduce-scatter.12
  604.8 41.7 all-gather.11
  673.0 78.2 reduce-scatter.14
  753.9 41.7 all-gather.13
  822.2 78.2 reduce-scatter.16
  904.1 101.3 all-reduce.2
where the time goes:
time: 1040 us; the launch traced here: 1030 us
  waiting for transfers between devices  722 us (69%)
  blocking collectives  127 us (12%)
  matrix products  103 us (10%)
  local copies, waits for them, and re-layouts  51.7 us (5%)
  between operations  15.5 us (1%)
  other arithmetic  13.9 us (1%)
    reduce_scatter x6, waiting for transfers between devices, body(): lax.psum_scatter(jnp.einsum('nt,rtf->rnf', dense_hot, pushed, precision=h...  390 us
    all_gather x5, waiting for transfers between devices, body(): every_firm = lax.all_gather(firm_round, 'tiles', axis=1, tiled=True)  230 us
    unnamed x1, blocking collectives  110 us
    psum x1, waiting for transfers between devices, body(): summed = lax.psum(local_term, 'tiles')  102 us
    dot_general x5, matrix products, body(): jnp.einsum('twf,rtf->rtw', tiles_w, tile_firm, preferred_element_type=jnp...  28.7 us
    dot_general x6, matrix products, body(): jnp.einsum('nt,rtf->rnf', dense_hot, pushed, precision=highest)  24.9 us
    dot_general x6, matrix products, body(): jnp.einsum('twf,rtw->rtf', tiles_w, tile_values, preferred_element_type=j...  24.6 us
  transfers between devices with their start and end apart: 12, of which 11 were waited for; matrix products, arithmetic and copies ran while one was open for 1% of the time, Pallas kernels for 0%

commit v1 on v0

--- a/solution.py
+++ b/solution.py
@@ -103,7 +103,15 @@
         firm_older, firm_newer = (firm_newer, firm_now)
         if sweep_index + 1 < SWEEPS:
             firm_round = firm_now.astype(jnp.bfloat16)
-            every_firm = lax.all_gather(firm_round, "tiles", axis=1, tiled=True)
+            every_firm = jnp.concatenate(
+                lax.all_to_all(
+                    jnp.stack([firm_round] * lax.psum(1, axis_name="tiles")),
+                    concat_axis=0,
+                    axis_name="tiles",
+                    split_axis=0,
+                ),
+                axis=1,
+            )
             tile_firm = jnp.take(every_firm, tile_block, axis=1)
     worker_effect = worker_now.reshape(replicas_here, WORK_BLOCKS * tile_cells)
     firm_flat = firm_now.reshape(replicas_here, FIRM_BLOCKS * tile_cells)

time: 1040 us -> 935 us (0.90)
  waiting for transfers between devices: 722 us -> 506 us
  blocking collectives: 127 us -> 211 us
  starting transfers between devices: 0.68 us -> 23.4 us
    all_gather x5 -> x0, waiting for transfers between devices: 230 us -> none  [body(): every_firm = lax.all_gather(firm_round, 'tiles', axis=1, tiled=True)]
    all_to_all x0 -> x4, blocking collectives: none -> 84 us  [body(): lax.all_to_all(jnp.stack([firm_round] * lax.psum(1, axis_name='tiles')),...]
    all_to_all x0 -> x1, starting transfers between devices: none -> 22.9 us  [body(): lax.all_to_all(jnp.stack([firm_round] * lax.psum(1, axis_name='tiles')),...]
    all_to_all x0 -> x1, waiting for transfers between devices: none -> 14.7 us  [body(): lax.all_to_all(jnp.stack([firm_round] * lax.psum(1, axis_name='tiles')),...]
  transfers between devices with their start and end apart: 12 -> 8, of which waited for: 11 -> 7; matrix products, arithmetic and copies ran while one was open for 1% -> 1% of each run, Pallas kernels for 0% -> 0%
where the time goes in v1:
time: 935 us; the launch traced here: 927 us
  waiting for transfers between devices  506 us (54%)
  blocking collectives  211 us (23%)
  matrix products  103 us (11%)
  local copies, waits for them, and re-layouts  57.4 us (6%)
  starting transfers between devices  23.4 us (3%)
  between operations  15.7 us (2%)
  other arithmetic  10.8 us (1%)
    reduce_scatter x6, waiting for transfers between devices, body(): lax.psum_scatter(jnp.einsum('nt,rtf->rnf', dense_hot, pushed, precision=h...  389 us
    unnamed x1, blocking collectives  110 us
    psum x1, waiting for transfers between devices, body(): summed = lax.psum(local_term, 'tiles')  102 us
    all_to_all x4, blocking collectives, body(): lax.all_to_all(jnp.stack([firm_round] * lax.psum(1, axis_name='tiles')),...  84 us
    dot_general x5, matrix products, body(): jnp.einsum('twf,rtf->rtw', tiles_w, tile_firm, preferred_element_type=jnp...  28.8 us
    transpose x6, local copies, waits for them, and re-layouts, body(): jnp.einsum('nt,rtf->rnf', dense_hot, pushed, precision=highest)  26.2 us
    dot_general x6, matrix products, body(): jnp.einsum('nt,rtf->rnf', dense_hot, pushed, precision=highest)  24.9 us
    dot_general x6, matrix products, body(): jnp.einsum('twf,rtw->rtf', tiles_w, tile_values, preferred_element_type=j...  24.6 us
  transfers between devices with their start and end apart: 8, of which 7 were waited for; matrix products, arithmetic and copies ran while one was open for 1% of the time, Pallas kernels for 0%

profile of v1, /device:TPU:6, one launch (start us, length us, event | category | flops | bytes accessed | tf_op | source)
XLA Modules:
  0.0 926.9 jit_solution(12816127627307912274)
XLA Ops:
  16.6 4.2 fusion.56
  28.9 109.8 %all-reduce = f32[64,128]{1,0:T(8,128)S(1)} all-reduce(f32[64,128]{1,0:T(8,128)S(1)} %fusion.164), channel_id=3, replica_groups=mesh['tiles'=32,'reps'=4] {'tiles'}, use_global_device_ids=true, to_apply=%region_3.0.clone | all-reduce | flops 8192 | bytes 65536
  141.0 22.9 %all-to-all-start = ((bf16[32,64,2,128]{3,1,2,0:T(8,128)(2,1)}), bf16[32,64,2,128]{3,1,2,0:T(8,128)(2,1)S(1)}, u32[]{:S(2)}, u32[]{:S(2)}) async-start(bf16[32,64,2,128]{3,1,2,0:T(8,128)(2,1)} %stack.10), calls=%async_computation.1 | async-start | bytes 2097152 | tf_op jit(solution)/shard_map/all_to_all | solution.py:107
  164.4 14.7 %all-to-all-done = bf16[32,64,2,128]{3,1,2,0:T(8,128)(2,1)S(1)} async-done(((bf16[32,64,2,128]{3,1,2,0:T(8,128)(2,1)}), bf16[32,64,2,128]{3,1,2,0:T(8,128)(2,1)S(1)}, u32[]{:S(2)}, u32[]{:S(2)}) %all-to-all-start) | async-done | bytes 1048608 | tf_op jit(solution)/shard_map/all_to_all | solution.py:107
  181.2 5.8 convolution_bitcast_fusion.9
  201.3 12.4 %copy.94 = f32[64,64,128]{2,0,1:T(8,128)} copy(f32[64,64,128]{2,1,0:T(8,128)S(1)} %fusion.59) | data formatting | bytes 4194304 | tf_op jit(solution)/shard_map/nt,rtf->rnf/transpose | solution.py:96
  213.8 79.1 %reduce-scatter.9.cloned.1.call-done = f32[64,2,128]{2,0,1:T(8,128)} async-done(((f32[64,64,128]{2,0,1:T(8,128)}), f32[64,2,128]{2,0,1:T(8,128)}) %reduce-scatter.9.cloned.1.call-update) | async-done | bytes 65552 | tf_op jit(solution)/shard_map/reduce_scatter | solution.py:95
  294.0 21.0 %all_to_all.25 = bf16[32,64,2,128]{3,1,2,0:T(8,128)(2,1)S(1)} all-to-all(bf16[32,64,2,128]{3,1,2,0:T(8,128)(2,1)S(1)} %stack.11), channel_id=1, replica_groups=mesh['tiles'=32,'reps'=4] {'tiles'}, dimensions={0} | all-to-all | bytes 2097152 | tf_op jit(solution)/shard_map/all_to_all | solution.py:107
  317.1 5.8 convolution_bitcast_fusion.7
  333.0 4.2 fusion.62
  340.2 78.0 %reduce-scatter.11.cloned.1.call-done = f32[64,2,128]{2,0,1:T(8,128)} async-done(((f32[64,64,128]{2,0,1:T(8,128)}), f32[64,2,128]{2,0,1:T(8,128)}) %reduce-scatter.11.cloned.1.call-update) | async-done | bytes 65552 | tf_op jit(solution)/shard_map/reduce_scatter | solution.py:95
  419.3 21.0 %all_to_all.26 = bf16[32,64,2,128]{3,1,2,0:T(8,128)(2,1)S(1)} all-to-all(bf16[32,64,2,128]{3,1,2,0:T(8,128)(2,1)S(1)} %stack.12), channel_id=1, replica_groups=mesh['tiles'=32,'reps'=4] {'tiles'}, dimensions={0} | all-to-all | bytes 2097152 | tf_op jit(solution)/shard_map/all_to_all | solution.py:107
  442.5 5.8 convolution_bitcast_fusion.5
  458.4 4.2 fusion.65
  465.4 78.0 %reduce-scatter.13.cloned.1.call-done = f32[64,2,128]{2,0,1:T(8,128)} async-done(((f32[64,64,128]{2,0,1:T(8,128)}), f32[64,2,128]{2,0,1:T(8,128)}) %reduce-scatter.13.cloned.1.call-update) | async-done | bytes 65552 | tf_op jit(solution)/shard_map/reduce_scatter | solution.py:95
  544.4 21.0 %all_to_all.27 = bf16[32,64,2,128]{3,1,2,0:T(8,128)(2,1)S(1)} all-to-all(bf16[32,64,2,128]{3,1,2,0:T(8,128)(2,1)S(1)} %stack.13), channel_id=1, replica_groups=mesh['tiles'=32,'reps'=4] {'tiles'}, dimensions={0} | all-to-all | bytes 2097152 | tf_op jit(solution)/shard_map/all_to_all | solution.py:107
  567.6 5.8 convolution_bitcast_fusion.3
  590.5 77.9 %reduce-scatter.15.cloned.1.call-done = f32[64,2,128]{2,0,1:T(8,128)} async-done(((f32[64,64,128]{2,0,1:T(8,128)}), f32[64,2,128]{2,0,1:T(8,128)}) %reduce-scatter.15.cloned.1.call-update) | async-done | bytes 65552 | tf_op jit(solution)/shard_map/reduce_scatter | solution.py:95
  669.6 21.0 %all_to_all.28 = bf16[32,64,2,128]{3,1,2,0:T(8,128)(2,1)S(1)} all-to-all(bf16[32,64,2,128]{3,1,2,0:T(8,128)(2,1)S(1)} %stack.14), channel_id=1, replica_groups=mesh['tiles'=32,'reps'=4] {'tiles'}, dimensions={0} | all-to-all | bytes 2097152 | tf_op jit(solution)/shard_map/all_to_all | solution.py:107
  692.7 5.8 convolution_bitcast_fusion.1
  708.7 4.2 fusion.71
  717.7 75.9 %reduce-scatter.17.cloned.1.call-done = f32[64,2,128]{2,0,1:T(8,128)} async-done(((f32[64,64,128]{2,0,1:T(8,128)}), f32[64,2,128]{2,0,1:T(8,128)}) %reduce-scatter.17.cloned.1.call-update) | async-done | bytes 65552 | tf_op jit(solution)/shard_map/reduce_scatter | solution.py:95
  796.6 102.3 %all-reduce.3.cloned.1.call-done = f32[64,512]{1,0:T(8,128)} async-done(((f32[64,512]{1,0:T(8,128)}), f32[64,512]{1,0:T(8,128)}) %all-reduce.3.cloned.1.call-update) | async-done | bytes 131088 | tf_op jit(solution)/shard_map/psum | solution.py:120
  900.2 17.3 %psum.15 = f32[16,512]{1,0:T(8,128)S(1)} all-reduce(f32[16,512]{1,0:T(8,128)S(1)} %fusion.162), channel_id=1, replica_groups=mesh['tiles'=32,'reps'=4] {'reps'}, use_global_device_ids=true, to_apply=%region_11.14 | all-reduce | flops 8192 | bytes 65536 | tf_op jit(solution)/shard_map/psum | solution.py:126
  (109 shorter events, 113.8 us)
Async XLA Ops:
  7.2 708.6 %copy-start = (f32[512,512]{1,0:T(8,128)S(1)}, f32[512,512]{1,0:T(8,128)}, u32[]{:S(2)}) copy-start(f32[512,512]{1,0:T(8,128)} %param.29) | copy-start | bytes 3145732
  7.2 3.1 copy-start.11
  7.2 3.1 copy-start.6
  7.2 131.7 %reduce-scatter.7.cloned.1.call-start = ((), (), s32[]{:S(2)}) async-start(), calls=%async_computation.11 | async-start | bytes 2162688 | tf_op jit(solution)/shard_map/reduce_scatter | solution.py:95
  23.3 0.7 copy-start.12
  25.2 113.4 %copy-start.7 = (s32[64,256]{1,0:T(8,128)S(1)}, s32[64,256]{1,0:T(8,128)}, u32[]{:S(2)}) copy-start(s32[64,256]{1,0:T(8,128)} %param.27) | copy-start | bytes 196612
  25.2 113.4 %copy-start.8 = (s32[256]{0:T(256)S(1)}, s32[256]{0:T(256)}, u32[]{:S(2)}) copy-start(s32[256]{0:T(256)} %param.26) | copy-start | bytes 3076
  25.3 113.4 %copy-start.9 = (f32[256]{0:T(256)S(1)}, f32[256]{0:T(256)}, u32[]{:S(2)}) copy-start(f32[256]{0:T(256)} %param.25) | copy-start | bytes 3076
  25.3 113.4 %copy-start.10 = (f32[256]{0:T(256)S(1)}, f32[256]{0:T(256)}, u32[]{:S(2)}) copy-start(f32[256]{0:T(256)} %param.24) | copy-start | bytes 3076
  28.7 135.5 %copy-start.5 = (s32[128]{0:T(128)S(1)}, s32[128]{0:T(128)}, u32[]{:S(2)}) copy-start(s32[128]{0:T(128)} %param.18) | copy-start | bytes 1540
  141.0 38.1 %all-to-all-start = ((bf16[32,64,2,128]{3,1,2,0:T(8,128)(2,1)}), bf16[32,64,2,128]{3,1,2,0:T(8,128)(2,1)S(1)}, u32[]{:S(2)}, u32[]{:S(2)}) async-start(bf16[32,64,2,128]{3,1,2,0:T(8,128)(2,1)} %stack.10), calls=%async_computation.1 | async-start | bytes 2097152 | tf_op jit(solution)/shard_map/all_to_all | solution.py:107
  163.9 129.0 %reduce-scatter.9.cloned.1.call-start = ((), (), s32[]{:S(2)}) async-start(), calls=%async_computation.12 | async-start | bytes 2162688 | tf_op jit(solution)/shard_map/reduce_scatter | solution.py:95
  213.7 204.5 %reduce-scatter.11.cloned.1.call-start = ((), (), s32[]{:S(2)}) async-start(), calls=%async_computation.13 | async-start | bytes 2162688 | tf_op jit(solution)/shard_map/reduce_scatter | solution.py:95
  340.2 78.0 %copy-start.2 = (f32[64,2,128]{2,0,1:T(8,128)S(1)}, f32[64,2,128]{2,0,1:T(8,128)}, u32[]{:S(2)}) copy-start(f32[64,2,128]{2,0,1:T(8,128)} %reduce-scatter.7.cloned.1.call-done) | copy-start | bytes 196612
  340.2 203.1 %reduce-scatter.13.cloned.1.call-start = ((), (), s32[]{:S(2)}) async-start(), calls=%async_computation.14 | async-start | bytes 2162688 | tf_op jit(solution)/shard_map/reduce_scatter | solution.py:95
  465.3 78.0 %copy-start.3 = (f32[64,2,128]{2,0,1:T(8,128)S(1)}, f32[64,2,128]{2,0,1:T(8,128)}, u32[]{:S(2)}) copy-start(f32[64,2,128]{2,0,1:T(8,128)} %reduce-scatter.9.cloned.1.call-done) | copy-start | bytes 196612
  465.3 203.2 %reduce-scatter.15.cloned.1.call-start = ((), (), s32[]{:S(2)}) async-start(), calls=%async_computation.15 | async-start | bytes 2162688 | tf_op jit(solution)/shard_map/reduce_scatter | solution.py:95
  590.5 203.2 %reduce-scatter.17.cloned.1.call-start = ((), (), s32[]{:S(2)}) async-start(), calls=%async_computation.16 | async-start | bytes 2162688 | tf_op jit(solution)/shard_map/reduce_scatter | solution.py:95
  715.6 1.0 copy-start.1
  715.7 183.2 %all-reduce.3.cloned.1.call-start = ((), (), s32[]{:S(2)}) async-start(), calls=%async_computation.17 | async-start | bytes 262144 | tf_op jit(solution)/shard_map/psum | solution.py:120
  794.6 125.1 %copy-start.4 = (f32[64,256]{1,0:T(8,128)}, f32[64,256]{1,0:T(8,128)S(1)}, u32[]{:S(2)}) copy-start(f32[64,256]{1,0:T(8,128)S(1)} %copy_bitcast_fusion.1) | copy-start | bytes 196612
Sparse Core Ops, SparseCore 0:
  23.5 80.8 reduce-scatter.6
  213.9 78.9 reduce-scatter.8
  340.3 77.8 reduce-scatter.10
  465.4 77.8 reduce-scatter.12
  590.6 77.8 reduce-scatter.14
  715.8 77.8 reduce-scatter.16
  797.5 101.3 all-reduce.2
